TPU v7x, 32 devices: a whole 2x2x4 slice. The times are simulated.
32 devices in a mesh: rep: 8 (over y, x, core), sp: 4 (over z).
Axes of the slice: x: 2, y: 2, z: 4, core: 2. Of those that a mesh axis runs over, the one named last changes fastest.
Arguments:
- field: bfloat16 [8, 128, 100, 128], P('rep', 'sp'), may hold values from -6 to 6
- send_blocks: int32 [4, 4, 8], P('sp'), may hold values from 0 to 31
- send_count: int32 [4, 4], P('sp'), may hold values from 1 to 8, as said below
- regrid_weights: bfloat16 [32, 8, 128, 128], P('sp'), may hold values from -0.1875 to 0.1875
- tile_slot: int32 [32, 8], P('sp'), may hold values from 0 to 31
- edge_inputs: bfloat16 [12288, 1536], P(('rep', 'sp')), may hold values from -6 to 6
- cotangent: bfloat16 [12288, 512], P(('rep', 'sp')), may hold values from -0.15625 to 0.15625
Outputs:
- hidden: bfloat16 [8, 32, 100, 128], P('rep', 'sp')
- weight_grad: float32 [1536, 512], P(('rep', 'sp'))
Inputs may be any that keep to these rules, and one draw needn't show every extreme that they name: `send_count`: every count is at most 8, and some pair of shards has exactly 8 in every draw.
All inputs are finite; a program needn't handle non-finite values.
Results may differ from a plain program's by a relative error of at most 0.001.
Values may be sent and summed in bfloat16 or wider, within the bound.
A program may use at most 64 MiB of HBM per device.

v0:
```python
import jax
import jax.numpy as jnp
from jax import lax
from jax.sharding import PartitionSpec as P


def body(field, send_blocks, send_count, regrid_weights, tile_slot, edge_inputs, cotangent):
    sample = field[0]
    own_lists = send_blocks[0]
    shards = own_lists.shape[0]
    slots_each = own_lists.shape[1]
    channels = sample.shape[1]
    cells = sample.shape[2]
    alive = jnp.arange(slots_each, dtype=jnp.int32)[None, :] < send_count[0][:, None]
    outgoing = jnp.where(alive[:, :, None, None], sample[own_lists], jnp.zeros((), jnp.bfloat16))
    incoming = lax.all_to_all(outgoing, "sp", split_axis=0, concat_axis=0, tiled=True)
    block_pool = incoming.reshape(shards * slots_each, channels, cells)
    picked = block_pool[tile_slot]
    hidden = jnp.einsum(
        "tbcx,tbxn->tcn", picked, regrid_weights, preferred_element_type=jnp.float32
    )
    hidden = hidden.astype(jnp.bfloat16)[None]
    partial_value = lax.psum_scatter(
        lax.dot_general(
            edge_inputs, cotangent, (((0,), (0,)), ((), ())), preferred_element_type=jnp.float32
        ),
        "rep",
        scatter_dimension=0,
        tiled=True,
    )
    weight_grad = lax.psum_scatter(partial_value, "sp", scatter_dimension=0, tiled=True)
    return (hidden, weight_grad)


def solution(mesh):
    in_specs = (
        P("rep", "sp", None, None),
        P("sp", None, None),
        P("sp", None),
        P("sp", None, None, None),
        P("sp", None),
        P(("rep", "sp"), None),
        P(("rep", "sp"), None),
    )
    out_specs = (P("rep", "sp", None, None), P(("rep", "sp"), None))
    return jax.shard_map(body, mesh=mesh, in_specs=in_specs, out_specs=out_specs, check_vma=False)
```

profile of v0, /device:TPU:0, one launch (start us, length us, event | category | flops | bytes accessed | tf_op | source)
XLA Modules:
  0.0 90.9 jit_solution(5322619930155869061)
XLA Ops:
  7.2 0.0 copy-start
  7.2 0.0 reduce-scatter.3.cloned.1.call-start
  7.2 4.1 %fusion.2 = f32[1536,512]{1,0:T(8,128)} fusion(bf16[384,1536]{1,0:T(8,128)(2,1)} %param.12, bf16[384,512]{1,0:T(8,128)(2,1)} %param.13), kind=kOutput, calls=%fused_computation.12 | convolution fusion | flops 603979776 | bytes 4718592 | tf_op jit(solution)/shard_map/dot_general | solution.py:24
  11.4 0.0 reduce-scatter.3.cloned.1.call-update
  11.4 0.7 copy-done.3
  12.1 0.1 reshape.62
  12.1 0.4 copy-done.1
  12.5 1.2 %copy.19 = bf16[1,32,100,128]{3,2,1,0:T(8,128)(2,1)} copy(bf16[1,32,100,128]{3,1,2,0:T(8,128)(2,1)S(1)} %copy-done.1) | data formatting | bytes 1638400 | tf_op args[0]
  13.8 1.9 %gather_fusion = bf16[32,100,128]{2,1,0:T(8,128)(2,1)S(1)} fusion(bf16[32,100,128]{2,1,0:T(8,128)(2,1)} %bitcast.27, s32[1024]{0:T(1024)S(1)} %pad_clamp_fusion.1), kind=kCustom, calls=%fused_computation | custom fusion | bytes 1638528 | tf_op jit(solution)/shard_map/gather | solution.py:15
  15.6 0.0 copy-done.4
  15.7 0.1 iota_compare_fusion
  15.7 1.0 %copy_select_fusion = bf16[4,8,100,128]{3,1,2,0:T(8,128)(2,1)} fusion(bf16[4,8,100,128]{3,2,1,0:T(8,128)(2,1)S(1)} %bitcast.26, pred[4,8]{1,0:T(4,128)(4,1)S(1)} %iota_compare_fusion), kind=kLoop, calls=%fused_computation.6 | loop fusion | flops 409600 | bytes 1638432 | tf_op jit(solution)/shard_map/jit(_where)/select_n | solution.py:15
  16.8 6.3 %all-to-all-start = ((bf16[4,8,100,128]{3,1,2,0:T(8,128)(2,1)}), bf16[4,8,100,128]{3,1,2,0:T(8,128)(2,1)}, u32[]{:S(2)}, u32[]{:S(2)}) async-start(bf16[4,8,100,128]{3,1,2,0:T(8,128)(2,1)} %copy_select_fusion), calls=%async_computation | async-start | bytes 1638400 | tf_op jit(solution)/shard_map/all_to_all | solution.py:16
  23.1 0.0 reduce-scatter.5.cloned.1.call-start
  23.1 37.2 %reduce-scatter.3.cloned.1.call-done = f32[192,512]{1,0:T(8,128)} async-done(((f32[1536,512]{1,0:T(8,128)}), f32[192,512]{1,0:T(8,128)}) %reduce-scatter.3.cloned.1.call-update) | async-done | bytes 393232 | tf_op jit(solution)/shard_map/reduce_scatter | solution.py:23
  60.3 0.0 reduce-scatter.5.cloned.1.call-update
  60.4 0.0 copy-done.2
  60.4 0.1 reshape.70
  60.5 0.0 all-to-all-done
  60.5 1.3 %copy.14 = bf16[4,8,100,128]{3,2,1,0:T(8,128)(2,1)S(1)} copy(bf16[4,8,100,128]{3,1,2,0:T(8,128)(2,1)} %all-to-all-done) | data formatting | bytes 1638400 | tf_op jit(solution)/shard_map/all_to_all | solution.py:16
  61.8 2.0 %gather_fusion.1 = bf16[64,100,128]{2,1,0:T(8,128)(2,1)} fusion(bf16[32,100,128]{2,1,0:T(8,128)(2,1)S(1)} %bitcast.24, s32[1024]{0:T(1024)S(1)} %pad_clamp_fusion), kind=kCustom, calls=%fused_computation.1 | custom fusion | bytes 3277056 | tf_op jit(solution)/shard_map/gather | solution.py:18
  63.8 2.1 %fusion.1 = bf16[1,8,100,128]{3,2,1,0:T(8,128)(2,1)S(1)} fusion(bf16[8,8,100,128]{3,2,1,0:T(8,128)(2,1)} %bitcast.25, bf16[8,8,128,128]{3,2,1,0:T(8,128)(2,1)S(1)} %copy-done), kind=kOutput, calls=%fused_computation.4 | convolution fusion | flops 209817600 | bytes 3940352 | tf_op jit(solution)/shard_map/tbcx,tbxn->tcn/dot_general | solution.py:19
  65.9 0.7 copy.15
  66.6 17.4 %reduce-scatter.5.cloned.1.call-done = f32[48,512]{1,0:T(8,128)} async-done(((f32[192,512]{1,0:T(8,128)}), f32[48,512]{1,0:T(8,128)}) %reduce-scatter.5.cloned.1.call-update) | async-done | bytes 98320 | tf_op jit(solution)/shard_map/reduce_scatter | solution.py:31
  (9 shorter events, 0.0 us)
Async XLA Ops:
  7.2 56.6 %copy-start = (bf16[8,8,128,128]{3,2,1,0:T(8,128)(2,1)S(1)}, bf16[8,8,128,128]{3,2,1,0:T(8,128)(2,1)}, u32[]{:S(2)}) copy-start(bf16[8,8,128,128]{3,2,1,0:T(8,128)(2,1)} %param.10) | copy-start | bytes 6291460
  7.2 53.2 %reduce-scatter.3.cloned.1.call-start = ((), (), s32[]{:S(2)}) async-start(), calls=%async_computation.3 | async-start | bytes 3538944 | tf_op jit(solution)/shard_map/reduce_scatter | solution.py:23
  11.4 0.7 copy-start.3
  11.4 1.2 %copy-start.1 = (bf16[1,32,100,128]{3,1,2,0:T(8,128)(2,1)S(1)}, bf16[1,32,100,128]{3,1,2,0:T(8,128)(2,1)}, u32[]{:S(2)}) copy-start(bf16[1,32,100,128]{3,1,2,0:T(8,128)(2,1)} %param.7) | copy-start | bytes 2457604
  12.1 3.6 %copy-start.4 = (s32[1,4]{1,0:T(1,128)S(1)}, s32[1,4]{1,0:T(1,128)}, u32[]{:S(2)}) copy-start(s32[1,4]{1,0:T(1,128)} %param.9) | copy-start | bytes 52
  15.7 44.6 %copy-start.2 = (s32[8,8]{1,0:T(8,128)S(1)}, s32[8,8]{1,0:T(8,128)}, u32[]{:S(2)}) copy-start(s32[8,8]{1,0:T(8,128)} %param.11) | copy-start | bytes 772
  16.8 43.7 %all-to-all-start = ((bf16[4,8,100,128]{3,1,2,0:T(8,128)(2,1)}), bf16[4,8,100,128]{3,1,2,0:T(8,128)(2,1)}, u32[]{:S(2)}, u32[]{:S(2)}) async-start(bf16[4,8,100,128]{3,1,2,0:T(8,128)(2,1)} %copy_select_fusion), calls=%async_computation | async-start | bytes 1638400 | tf_op jit(solution)/shard_map/all_to_all | solution.py:16
  23.1 60.9 %reduce-scatter.5.cloned.1.call-start = ((), (), s32[]{:S(2)}) async-start(), calls=%async_computation.4 | async-start | bytes 491520 | tf_op jit(solution)/shard_map/reduce_scatter | solution.py:31
Sparse Core Ops, SparseCore 0:
  11.5 48.7 reduce-scatter.2
  63.2 20.7 reduce-scatter.4
where the time goes:
time: 91.2 us; the launch traced here: 90.9 us
  waiting for transfers between devices  54.7 us (60%)
  between operations  14.1 us (15%)
  local copies, waits for them, and re-layouts  8.31 us (9%)
  starting transfers between devices  6.39 us (7%)
  matrix products  6.26 us (7%)
  other arithmetic  1.12 us (1%)
    reduce_scatter x1, waiting for transfers between devices, body(): lax.psum_scatter(lax.dot_general(edge_inputs, cotangent, (((0,), (0,)), (...  37.2 us
    reduce_scatter x1, waiting for transfers between devices, body(): lax.psum_scatter(partial_value, 'sp', scatter_dimension=0, tiled=True)  17.4 us
    all_to_all x1, starting transfers between devices, body(): lax.all_to_all(outgoing, 'sp', split_axis=0, concat_axis=0, tiled=True)  6.35 us
    dot_general x1, matrix products, body(): lax.dot_general(edge_inputs, cotangent, (((0,), (0,)), ((), ())), preferr...  4.15 us
    unnamed x12, local copies, waits for them, and re-layouts  3 us
    dot_general x1, matrix products, body(): jnp.einsum('tbcx,tbxn->tcn', picked, regrid_weights, preferred_element_ty...  2.12 us
    gather x1, local copies, waits for them, and re-layouts, body(): picked = block_pool[tile_slot]  1.99 us
    gather x1, local copies, waits for them, and re-layouts, body(): sample[own_lists]  1.87 us
  transfers between devices with their start and end apart: 3, of which 2 were waited for; matrix products, arithmetic and copies ran while one was open for 12% of the time, Pallas kernels for 0%

commit v1 on v0

--- a/solution.py
+++ b/solution.py
@@ -1,7 +1,13 @@
+import functools
+
 import jax
 import jax.numpy as jnp
 from jax import lax
+from jax.experimental import pallas as pl
+from jax.experimental.pallas import tpu as pltpu
 from jax.sharding import PartitionSpec as P
+
+MESH = pl.DeviceIdType.MESH
 
 
 def body(field, send_blocks, send_count, regrid_weights, tile_slot, edge_inputs, cotangent):
@@ -32,6 +38,190 @@
     return (hidden, weight_grad)
 
 
+def kernel(
+    n_sp, lists, counts, slots, field_hbm, weights_hbm, edge_hbm, cot_hbm,
+    hidden_out, grad_out,
+    field, weights, edge, cot, outgoing, pool, part, got1, got2, got3, gotz,
+    load_sem, a2a_send, a2a_recv, s1, r1, s2, r2, s3, r3, sz, rz,
+):
+    rep = lax.axis_index("rep")
+    me = lax.axis_index("sp")
+    core = rep % 2
+    x = (rep // 2) % 2
+    y = rep // 4
+    w1, w2 = 1 + core, 2 - core
+    b1 = x + core * (y - x)
+    b2 = y + core * (x - y)
+    twin = rep + 1 - 2 * core
+    first = rep + (1 - 2 * b1) * 2 * w1
+    second = rep + (1 - 2 * b2) * 2 * w2
+    blocks = field_hbm.shape[1]
+    slots_each = lists.shape[2]
+    tiles, reads = slots.shape
+    width = edge_hbm.shape[1] // 4
+    rows = part.shape[3]
+
+    loads = [
+        pltpu.make_async_copy(field_hbm.at[0], field.at[pl.ds(0, blocks)], load_sem.at[0]),
+        pltpu.make_async_copy(edge_hbm, edge, load_sem.at[1]),
+        pltpu.make_async_copy(cot_hbm, cot, load_sem.at[2]),
+        pltpu.make_async_copy(weights_hbm, weights, load_sem.at[3]),
+    ]
+    for load in loads:
+        load.start()
+
+    barrier = pltpu.get_barrier_semaphore()
+    sp_peers = [lax.rem(me + k, n_sp) for k in range(1, n_sp)]
+    for peer in sp_peers:
+        pl.semaphore_signal(barrier, inc=1, device_id=(rep, peer), device_id_type=MESH)
+    for peer in (twin, first, second):
+        pl.semaphore_signal(barrier, inc=1, device_id=(peer, me), device_id_type=MESH)
+
+    field[blocks] = jnp.zeros(field.shape[1:], field.dtype)
+    loads[0].wait()
+    pl.semaphore_wait(barrier, n_sp - 1 + 3)
+
+    def block_for(d, j):
+        return field[jnp.where(j < counts[0, d], lists[0, d, j], blocks)]
+
+    def send(src, dst, ssem, rsem, device):
+        copy = pltpu.make_async_remote_copy(
+            src_ref=src, dst_ref=dst, send_sem=ssem, recv_sem=rsem,
+            device_id=device, device_id_type=MESH,
+        )
+        copy.start()
+        return copy
+
+    a2a = []
+    for k in range(n_sp - 1):
+        for j in range(slots_each):
+            outgoing[k, j] = block_for(sp_peers[k], j)
+        a2a.append(send(
+            outgoing.at[k], pool.at[pl.ds(me * slots_each, slots_each)],
+            a2a_send.at[k], a2a_recv.at[k], (rep, sp_peers[k]),
+        ))
+
+    def chunk(flip1, flip2):
+        return (b1 + flip1 * (1 - 2 * b1)) * w1 + (b2 + flip2 * (1 - 2 * b2)) * w2
+
+    loads[1].wait()
+    loads[2].wait()
+    to_twin = []
+    for k, (f1, f2) in enumerate(((1, 1), (0, 1), (1, 0), (0, 0))):
+        q = chunk(f1, f2)
+        columns = pl.ds(pl.multiple_of(q * width, 128), width)
+        value = lax.dot_general(
+            edge[:, columns], cot[...], (((0,), (0,)), ((), ())),
+            preferred_element_type=jnp.float32,
+        )
+        part[q] = value.reshape(part.shape[1:])
+        to_twin.append(send(
+            part.at[q, 1 - core], got1.at[k], s1.at[k], r1.at[k], (twin, me)
+        ))
+    for j in range(slots_each):
+        pool[me * slots_each + j] = block_for(me, j)
+
+    order = sp_peers + [me]
+    c_both, c_first, c_second, c_none = chunk(1, 1), chunk(1, 0), chunk(0, 1), chunk(0, 0)
+
+    def fold(q, k):
+        to_twin[k].wait_recv()
+        part[q, core] = part[q, core] + got1[k]
+
+    out2 = []
+    for k, q in enumerate((c_both, c_first)):
+        fold(q, k)
+        for i in range(n_sp):
+            out2.append(send(
+                part.at[q, core, order[i]], got2.at[k, order[i]],
+                s2.at[k, i], r2.at[k, i], (first, me),
+            ))
+    fold(c_second, 2)
+    fold(c_none, 3)
+    out3 = []
+    for i in range(n_sp):
+        out2[i].wait_recv()
+        part[c_second, core, order[i]] = part[c_second, core, order[i]] + got2[0, order[i]]
+        out3.append(send(
+            part.at[c_second, core, order[i]], got3.at[order[i]],
+            s3.at[i], r3.at[i], (second, me),
+        ))
+    outz = []
+    for i in range(n_sp):
+        out2[n_sp + i].wait_recv()
+        out3[i].wait_recv()
+        total = part[c_none, core, order[i]] + got2[1, order[i]] + got3[order[i]]
+        part[c_none, core, order[i]] = total
+        if i < n_sp - 1:
+            outz.append(send(
+                part.at[c_none, core, order[i]], gotz.at[i], sz.at[i], rz.at[i], (rep, order[i])
+            ))
+
+    for copy in a2a:
+        copy.wait_recv()
+    loads[3].wait()
+    for t in range(tiles):
+        left = jnp.concatenate([pool[slots[t, b]] for b in range(reads)], axis=1)
+        right = weights[t].reshape(reads * weights.shape[2], weights.shape[3])
+        value = jnp.dot(left, right, preferred_element_type=jnp.float32)
+        hidden_out[0, t] = value.astype(hidden_out.dtype)
+
+    for copy in outz:
+        copy.wait_recv()
+    total = part[c_none, core, me]
+    for i in range(n_sp - 1):
+        total = total + gotz[i]
+    grad_out[...] = total
+    for copy in a2a + to_twin + out2 + out3 + outz:
+        copy.wait_send()
+
+
+def fused(mesh, field, send_blocks, send_count, regrid_weights, tile_slot, edge_inputs, cotangent):
+    n_sp = mesh.shape["sp"]
+    n_rep = mesh.shape["rep"]
+    _, blocks, channels, cells = field.shape
+    slots_each = send_blocks.shape[2]
+    tiles = tile_slot.shape[0]
+    n_in, hid = edge_inputs.shape[1], cotangent.shape[1]
+    rows = n_in // (n_rep * n_sp)
+    bf16, f32 = jnp.bfloat16, jnp.float32
+    dma = pltpu.SemaphoreType.DMA
+    smem = pl.BlockSpec(memory_space=pltpu.SMEM)
+    far = pl.BlockSpec(memory_space=pl.ANY)
+    near = pl.BlockSpec(memory_space=pltpu.VMEM)
+    return pl.pallas_call(
+        functools.partial(kernel, n_sp),
+        out_shape=(
+            jax.ShapeDtypeStruct((1, tiles, channels, regrid_weights.shape[3]), bf16),
+            jax.ShapeDtypeStruct((rows, hid), f32),
+        ),
+        in_specs=[smem, smem, smem, far, far, far, far],
+        out_specs=(near, near),
+        scratch_shapes=[
+            pltpu.VMEM((blocks + 1, channels, cells), bf16),
+            pltpu.VMEM(regrid_weights.shape, bf16),
+            pltpu.VMEM(edge_inputs.shape, bf16),
+            pltpu.VMEM(cotangent.shape, bf16),
+            pltpu.VMEM((n_sp - 1, slots_each, channels, cells), bf16),
+            pltpu.VMEM((n_sp * slots_each, channels, cells), bf16),
+            pltpu.VMEM((4, 2, n_sp, rows, hid), f32),
+            pltpu.VMEM((4, n_sp, rows, hid), f32),
+            pltpu.VMEM((2, n_sp, rows, hid), f32),
+            pltpu.VMEM((n_sp, rows, hid), f32),
+            pltpu.VMEM((n_sp - 1, rows, hid), f32),
+            dma((4,)),
+            dma((n_sp - 1,)), dma((n_sp - 1,)),
+            dma((4,)), dma((4,)),
+            dma((2, n_sp)), dma((2, n_sp)),
+            dma((n_sp,)), dma((n_sp,)),
+            dma((n_sp - 1,)), dma((n_sp - 1,)),
+        ],
+        compiler_params=pltpu.CompilerParams(
+            collective_id=0, has_side_effects=True, vmem_limit_bytes=56 * 1024 * 1024
+        ),
+    )(send_blocks, send_count, tile_slot, field, regrid_weights, edge_inputs, cotangent)
+
+
 def solution(mesh):
     in_specs = (
         P("rep", "sp", None, None),
@@ -43,4 +233,6 @@
         P(("rep", "sp"), None),
     )
     out_specs = (P("rep", "sp", None, None), P(("rep", "sp"), None))
-    return jax.shard_map(body, mesh=mesh, in_specs=in_specs, out_specs=out_specs, check_vma=False)
+    binary = mesh.shape["rep"] == 2 * 2 * 2
+    inner = functools.partial(fused, mesh) if binary else body
+    return jax.shard_map(inner, mesh=mesh, in_specs=in_specs, out_specs=out_specs, check_vma=False)

time: 91.2 us -> 40.2 us (0.44)
  waiting for transfers between devices: 54.7 us -> 0 us
  Pallas kernels: 0 us -> 33.8 us
  between operations: 14.1 us -> 0.64 us
  starting transfers between devices: 6.39 us -> 0 us
  matrix products: 6.26 us -> 0 us
  local copies, waits for them, and re-layouts: 8.31 us -> 5.55 us
  other arithmetic: 1.12 us -> 0 us
    reduce_scatter x2 -> x0, waiting for transfers between devices: 54.7 us -> none  [the longest x1 37.2 us: body(): lax.psum_scatter(lax.dot_general(edge_inputs, cotangent, (((0,), (0,)), (...]
    pallas_call x0 -> x1, Pallas kernels: none -> 33.8 us  [fused(): pl.pallas_call(functools.partial(kernel, n_sp), out_shape=(jax.ShapeDtype...]
    all_to_all x1 -> x0, starting transfers between devices: 6.35 us -> none  [body(): lax.all_to_all(outgoing, 'sp', split_axis=0, concat_axis=0, tiled=True)]
    dot_general x2 -> x0, matrix products: 6.26 us -> none  [the longest x1 4.15 us: body(): lax.dot_general(edge_inputs, cotangent, (((0,), (0,)), ((), ())), preferr...]
    gather x2 -> x0, local copies, waits for them, and re-layouts: 3.87 us -> none  [the longest x1 1.99 us: body(): picked = block_pool[tile_slot]]
    pallas_call x0 -> x1, local copies, waits for them, and re-layouts: none -> 1.64 us  [fused(): pl.pallas_call(functools.partial(kernel, n_sp), out_shape=(jax.ShapeDtype...]
    all_to_all x1 -> x0, local copies, waits for them, and re-layouts: 1.27 us -> none  [body(): lax.all_to_all(outgoing, 'sp', split_axis=0, concat_axis=0, tiled=True)]
    select_n x3 -> x0, other arithmetic: 1.04 us -> none  [the longest x1 1.03 us: body(): jnp.where(alive[:, :, None, None], sample[own_lists], jnp.zeros((), jnp.b...]
  transfers between devices with their start and end apart: 3 -> 0, of which waited for: 2 -> 0; matrix products, arithmetic and copies ran while one was open for 12% -> 0% of each run, Pallas kernels for 0% -> 0%
where the time goes in v1:
time: 40.2 us; the launch traced here: 40 us
  Pallas kernels  33.8 us (84%)
  local copies, waits for them, and re-layouts  5.55 us (14%)
  between operations  0.64 us (2%)
    pallas_call x1, Pallas kernels, fused(): pl.pallas_call(functools.partial(kernel, n_sp), out_shape=(jax.ShapeDtype...  33.8 us
    unnamed x2, local copies, waits for them, and re-layouts  3.91 us
    pallas_call x1, local copies, waits for them, and re-layouts, fused(): pl.pallas_call(functools.partial(kernel, n_sp), out_shape=(jax.ShapeDtype...  1.64 us

profile of v1, /device:TPU:0, one launch (start us, length us, event | category | flops | bytes accessed | tf_op | source)
XLA Modules:
  0.0 40.0 jit_solution(7396595388159465524)
XLA Ops:
  0.6 2.4 %copy.9.field_hbm = bf16[1,32,100,128]{3,2,1,0:T(8,128)(2,1)} copy(bf16[1,32,100,128]{3,1,2,0:T(8,128)(2,1)} %param.7) | data formatting | bytes 1638400 | tf_op args[0]
  3.0 33.8 %shard_map.86 = (bf16[1,8,100,128]{3,2,1,0:T(8,128)(2,1)}, f32[48,512]{1,0:T(8,128)}) custom-call(s32[1,4,8]{2,1,0:T(4,128)} %lists.1, s32[1,4]{1,0:T(1,128)} %counts.1, s32[8,8]{1,0:T(8,128)} %slots.1, bf16[1,32,100,128]{3,2,1,0:T(8,128)(2,1)} %copy.9.field_hbm, bf16[8,8,128,128]{3,2,1,0:T(8,128)(2,1)} %weights_hbm.1, bf16[384,1536]{1,0:T(8,128)(2,1)} %edge_hbm.1, ...), custom_call_target="tpu_custom_call" | custom-call | tf_op jit(solution)/shard_map/pallas_call | solution.py:192
  36.8 1.6 %copy.10 = bf16[1,8,100,128]{3,1,2,0:T(8,128)(2,1)} copy(bf16[1,8,100,128]{3,2,1,0:T(8,128)(2,1)} %get-tuple-element.2) | data formatting | bytes 409600 | tf_op jit(solution)/shard_map/pallas_call | solution.py:192
  38.4 1.5 %copy.12 = f32[48,512]{1,0:T(8,128)} copy(f32[48,512]{1,0:T(8,128)} %get-tuple-element.7) | data formatting | bytes 196608

commit v2 on v1

v2 whole, which is shorter than its diff:
```python
import jax
import jax.numpy as jnp
from jax import lax
from jax.experimental import pallas as pl
from jax.experimental.pallas import tpu as pltpu
from jax.sharding import PartitionSpec as P

MESH = pl.DeviceIdType.MESH


def body(field, send_blocks, send_count, regrid_weights, tile_slot, edge_inputs, cotangent):
    sample = field[0]
    own_lists = send_blocks[0]
    shards = own_lists.shape[0]
    slots_each = own_lists.shape[1]
    channels = sample.shape[1]
    cells = sample.shape[2]
    alive = jnp.arange(slots_each, dtype=jnp.int32)[None, :] < send_count[0][:, None]
    outgoing = jnp.where(alive[:, :, None, None], sample[own_lists], jnp.zeros((), jnp.bfloat16))
    incoming = lax.all_to_all(outgoing, "sp", split_axis=0, concat_axis=0, tiled=True)
    block_pool = incoming.reshape(shards * slots_each, channels, cells)
    picked = block_pool[tile_slot]
    hidden = jnp.einsum(
        "tbcx,tbxn->tcn", picked, regrid_weights, preferred_element_type=jnp.float32
    )
    hidden = hidden.astype(jnp.bfloat16)[None]
    partial_value = lax.psum_scatter(
        lax.dot_general(
            edge_inputs, cotangent, (((0,), (0,)), ((), ())), preferred_element_type=jnp.float32
        ),
        "rep",
        scatter_dimension=0,
        tiled=True,
    )
    weight_grad = lax.psum_scatter(partial_value, "sp", scatter_dimension=0, tiled=True)
    return (hidden, weight_grad)


def kernel(
    lists, counts, slots, field_hbm, weights_hbm, edge_hbm, cot_hbm,
    hidden_out, grad_out,
    field, wide, weights, edge, cot, outgoing, pool, tall, part, got1, got2, got3, gotz, gotf,
    load_sem, a2a_send, a2a_recv, s1, r1, s2, r2, s3, r3, sz, rz, sf, rf,
):
    rep = lax.axis_index("rep")
    me = lax.axis_index("sp")
    core = rep % 2
    x = (rep // 2) % 2
    y = rep // 4
    w1, w2 = 1 + core, 2 - core
    b1 = x + core * (y - x)
    b2 = y + core * (x - y)
    twin = rep + 1 - 2 * core
    first = rep + (1 - 2 * b1) * 2 * w1
    second = rep + (1 - 2 * b2) * 2 * w2
    low, high = me % 2, me // 2
    near = 2 * high + 1 - low
    far = 2 * (1 - high) + low
    diag = 2 * (1 - high) + 1 - low
    channels, blocks, cells = field.shape
    slots_each = lists.shape[2]
    tiles, reads = slots.shape
    width = edge_hbm.shape[1] // 4

    loads = [
        pltpu.make_async_copy(field_hbm.at[0], field, load_sem.at[0]),
        pltpu.make_async_copy(edge_hbm, edge, load_sem.at[1]),
        pltpu.make_async_copy(cot_hbm, cot, load_sem.at[2]),
        pltpu.make_async_copy(weights_hbm, weights, load_sem.at[3]),
    ]
    for load in loads:
        load.start()

    barrier = pltpu.get_barrier_semaphore()
    sp_peers = [far, diag, near]
    for peer in sp_peers:
        pl.semaphore_signal(barrier, inc=1, device_id=(rep, peer), device_id_type=MESH)
    for peer in (twin, first, second):
        pl.semaphore_signal(barrier, inc=1, device_id=(peer, me), device_id_type=MESH)

    loads[0].wait()
    wide[...] = field[...].astype(jnp.float32).reshape(wide.shape)

    def block_for(d, j):
        block = wide[pl.ds(lists[0, d, j], channels, stride=blocks), :]
        block = jnp.where(j < counts[0, d], block, jnp.zeros_like(block))
        return block.astype(jnp.bfloat16)

    def send(src, dst, ssem, rsem, device):
        copy = pltpu.make_async_remote_copy(
            src_ref=src, dst_ref=dst, send_sem=ssem, recv_sem=rsem,
            device_id=device, device_id_type=MESH,
        )
        copy.start()
        return copy

    a2a = []
    for k, peer in enumerate(sp_peers):
        for j in range(slots_each):
            outgoing[k, j] = block_for(peer, j)
        if k == 0:
            pl.semaphore_wait(barrier, 6)
        a2a.append(send(
            outgoing.at[k], pool.at[pl.ds(me * slots_each, slots_each)],
            a2a_send.at[k], a2a_recv.at[k], (rep, peer),
        ))

    def chunk(flip1, flip2):
        return (b1 + flip1 * (1 - 2 * b1)) * w1 + (b2 + flip2 * (1 - 2 * b2)) * w2

    loads[1].wait()
    loads[2].wait()
    to_twin = []
    for k, (f1, f2) in enumerate(((1, 1), (0, 1), (1, 0), (0, 0))):
        q = chunk(f1, f2)
        columns = pl.ds(pl.multiple_of(q * width, 128), width)
        value = lax.dot_general(
            edge[:, columns], cot[...], (((0,), (0,)), ((), ())),
            preferred_element_type=jnp.float32,
        )
        part[q] = value.reshape(part.shape[1:])
        to_twin.append(send(
            part.at[q, 1 - core], got1.at[k], s1.at[k], r1.at[k], (twin, me)
        ))
    for j in range(slots_each):
        pool[me * slots_each + j] = block_for(me, j)

    order = [diag, near, far, me]
    c_both, c_first, c_second, c_none = chunk(1, 1), chunk(1, 0), chunk(0, 1), chunk(0, 0)

    def fold(q, k):
        to_twin[k].wait_recv()
        part[q, core] = part[q, core] + got1[k]

    out2 = []
    for k, q in enumerate((c_both, c_first)):
        fold(q, k)
        for i in range(4):
            out2.append(send(
                part.at[q, core, order[i]], got2.at[k, order[i]],
                s2.at[k, i], r2.at[k, i], (first, me),
            ))
    fold(c_second, 2)
    fold(c_none, 3)
    out3 = []
    for i in range(4):
        out2[i].wait_recv()
        part[c_second, core, order[i]] = part[c_second, core, order[i]] + got2[0, order[i]]
        out3.append(send(
            part.at[c_second, core, order[i]], got3.at[order[i]],
            s3.at[i], r3.at[i], (second, me),
        ))
    outz = []
    for i in range(4):
        out2[4 + i].wait_recv()
        out3[i].wait_recv()
        total = part[c_none, core, order[i]] + got2[1, order[i]] + got3[order[i]]
        part[c_none, core, order[i]] = total
        if i < 2:
            outz.append(send(
                part.at[c_none, core, order[i]], gotz.at[i], sz.at[i], rz.at[i], (rep, near)
            ))
    outz[0].wait_recv()
    part[c_none, core, far] = part[c_none, core, far] + gotz[0]
    last = send(part.at[c_none, core, far], gotf, sf, rf, (rep, far))

    for copy in a2a:
        copy.wait_recv()
    loads[3].wait()
    for t in range(tiles):
        left = jnp.concatenate([pool[slots[t, b]] for b in range(reads)], axis=1)
        right = weights[t].reshape(reads * weights.shape[2], weights.shape[3])
        tall[pl.ds(t, channels, stride=tiles), :] = jnp.dot(
            left, right, preferred_element_type=jnp.float32
        )
    hidden_out[0] = tall[...].reshape(hidden_out.shape[1:]).astype(hidden_out.dtype)

    outz[1].wait_recv()
    total = part[c_none, core, me] + gotz[1]
    last.wait_recv()
    grad_out[...] = total + gotf[...]
    for copy in a2a + to_twin + out2 + out3 + outz + [last]:
        copy.wait_send()


def settle(hidden, grad, hidden_out, grad_out):
    hidden_out[...] = hidden[...]
    grad_out[...] = grad[...]


def fused(field, send_blocks, send_count, regrid_weights, tile_slot, edge_inputs, cotangent):
    _, blocks, channels, cells = field.shape
    slots_each = send_blocks.shape[2]
    tiles = tile_slot.shape[0]
    nodes = regrid_weights.shape[3]
    n_in, hid = edge_inputs.shape[1], cotangent.shape[1]
    rows = n_in // (lax.axis_size("rep") * lax.axis_size("sp"))
    bf16, f32 = jnp.bfloat16, jnp.float32
    dma = pltpu.SemaphoreType.DMA
    smem = pl.BlockSpec(memory_space=pltpu.SMEM)
    far = pl.BlockSpec(memory_space=pl.ANY)
    near = pl.BlockSpec(memory_space=pltpu.VMEM)
    out_shape = (
        jax.ShapeDtypeStruct((1, channels, tiles, nodes), bf16),
        jax.ShapeDtypeStruct((rows, hid), f32),
    )
    hidden, grad = pl.pallas_call(
        kernel,
        out_shape=out_shape,
        in_specs=[smem, smem, smem, far, far, far, far],
        out_specs=(near, near),
        scratch_shapes=[
            pltpu.VMEM((channels, blocks, cells), bf16),
            pltpu.VMEM((channels * blocks, cells), f32),
            pltpu.VMEM(regrid_weights.shape, bf16),
            pltpu.VMEM(edge_inputs.shape, bf16),
            pltpu.VMEM(cotangent.shape, bf16),
            pltpu.VMEM((3, slots_each, channels, cells), bf16),
            pltpu.VMEM((4 * slots_each, channels, cells), bf16),
            pltpu.VMEM((channels * tiles, nodes), f32),
            pltpu.VMEM((4, 2, 4, rows, hid), f32),
            pltpu.VMEM((4, 4, rows, hid), f32),
            pltpu.VMEM((2, 4, rows, hid), f32),
            pltpu.VMEM((4, rows, hid), f32),
            pltpu.VMEM((2, rows, hid), f32),
            pltpu.VMEM((rows, hid), f32),
            dma((4,)),
            dma((3,)), dma((3,)),
            dma((4,)), dma((4,)),
            dma((2, 4)), dma((2, 4)),
            dma((4,)), dma((4,)),
            dma((2,)), dma((2,)),
            dma, dma,
        ],
        compiler_params=pltpu.CompilerParams(
            collective_id=0, has_side_effects=True, vmem_limit_bytes=56 * 1024 * 1024
        ),
    )(
        send_blocks, send_count, tile_slot, jnp.transpose(field, (0, 2, 1, 3)),
        regrid_weights, edge_inputs, cotangent,
    )
    hidden, grad = pl.pallas_call(
        settle, out_shape=out_shape, in_specs=[near, near], out_specs=(near, near),
        compiler_params=pltpu.CompilerParams(vmem_limit_bytes=4 * 1024 * 1024),
    )(hidden, grad)
    return jnp.transpose(hidden, (0, 2, 1, 3)), grad


def solution(mesh):
    in_specs = (
        P("rep", "sp", None, None),
        P("sp", None, None),
        P("sp", None),
        P("sp", None, None, None),
        P("sp", None),
        P(("rep", "sp"), None),
        P(("rep", "sp"), None),
    )
    out_specs = (P("rep", "sp", None, None), P(("rep", "sp"), None))
    binary = mesh.shape["rep"] == 2 * 2 * 2 and mesh.shape["sp"] == 2 * 2
    inner = fused if binary else body
    return jax.shard_map(inner, mesh=mesh, in_specs=in_specs, out_specs=out_specs, check_vma=False)
```

time: 40.2 us -> 34.3 us (0.85)
  local copies, waits for them, and re-layouts: 5.55 us -> 1.82 us
  Pallas kernels: 33.8 us -> 31.6 us
    pallas_call x1 -> x2, Pallas kernels: 33.8 us -> 31.6 us  [the longest x1 30.9 us: fused(): pl.pallas_call(kernel, out_shape=out_shape, in_specs=[smem, smem, smem, f...]
    unnamed x2 -> x4, local copies, waits for them, and re-layouts: 3.91 us -> 1.82 us
    pallas_call x1 -> x0, local copies, waits for them, and re-layouts: 1.64 us -> none  [fused(): pl.pallas_call(functools.partial(kernel, n_sp), out_shape=(jax.ShapeDtype...]
where the time goes in v2:
time: 34.3 us; the launch traced here: 34.1 us
  Pallas kernels  31.6 us (92%)
  local copies, waits for them, and re-layouts  1.82 us (5%)
  between operations  0.65 us (2%)
    pallas_call x1, Pallas kernels, fused(): pl.pallas_call(kernel, out_shape=out_shape, in_specs=[smem, smem, smem, f...  30.9 us
    unnamed x4, local copies, waits for them, and re-layouts  1.82 us
    pallas_call x1, Pallas kernels, fused(): pl.pallas_call(settle, out_shape=out_shape, in_specs=[near, near], out_sp...  0.73 us

profile of v2, /device:TPU:0, one launch (start us, length us, event | category | flops | bytes accessed | tf_op | source)
XLA Modules:
  0.0 34.1 jit_solution(16542108872960511311)
XLA Ops:
  0.6 30.9 %shard_map.86 = (bf16[1,100,8,128]{3,2,1,0:T(8,128)(2,1)}, f32[48,512]{1,0:T(8,128)}) custom-call(s32[1,4,8]{2,1,0:T(4,128)} %lists.1, s32[1,4]{1,0:T(1,128)} %counts.1, s32[8,8]{1,0:T(8,128)} %slots.1, bf16[1,100,32,128]{3,2,1,0:T(8,128)(2,1)} %bitcast.2, bf16[8,8,128,128]{3,2,1,0:T(8,128)(2,1)} %weights_hbm.1, bf16[384,1536]{1,0:T(8,128)(2,1)} %edge_hbm.1, ...), custom_call_target="tpu_custom_call" | custom-call | tf_op jit(solution)/shard_map/pallas_call | solution.py:207
  31.5 0.0 copy-start
  31.5 0.9 %copy-done = bf16[1,100,8,128]{3,2,1,0:T(8,128)(2,1)S(1)} copy-done((bf16[1,100,8,128]{3,2,1,0:T(8,128)(2,1)S(1)}, bf16[1,100,8,128]{3,2,1,0:T(8,128)(2,1)}, u32[]{:S(2)}) %copy-start) | copy-done | bytes 204824
  32.4 0.0 copy-start.1
  32.4 0.9 %copy-done.1 = f32[48,512]{1,0:T(8,128)S(1)} copy-done((f32[48,512]{1,0:T(8,128)S(1)}, f32[48,512]{1,0:T(8,128)}, u32[]{:S(2)}) %copy-start.1) | copy-done | bytes 98328
  33.3 0.7 %shard_map.87 = (bf16[1,100,8,128]{3,2,1,0:T(8,128)(2,1)}, f32[48,512]{1,0:T(8,128)}) custom-call(bf16[1,100,8,128]{3,2,1,0:T(8,128)(2,1)S(1)} %copy-done, f32[48,512]{1,0:T(8,128)S(1)} %copy-done.1), custom_call_target="tpu_custom_call" | custom-call | tf_op jit(solution)/shard_map/pallas_call | solution.py:242
Async XLA Ops:
  31.5 0.9 %copy-start = (bf16[1,100,8,128]{3,2,1,0:T(8,128)(2,1)S(1)}, bf16[1,100,8,128]{3,2,1,0:T(8,128)(2,1)}, u32[]{:S(2)}) copy-start(bf16[1,100,8,128]{3,2,1,0:T(8,128)(2,1)} %get-tuple-element.6.hidden) | copy-start | bytes 614404
  32.4 0.9 %copy-start.1 = (f32[48,512]{1,0:T(8,128)S(1)}, f32[48,512]{1,0:T(8,128)}, u32[]{:S(2)}) copy-start(f32[48,512]{1,0:T(8,128)} %get-tuple-element.7.grad) | copy-start | bytes 294916

commit v3 on v2

--- a/solution.py
+++ b/solution.py
@@ -68,8 +68,8 @@
         pltpu.make_async_copy(cot_hbm, cot, load_sem.at[2]),
         pltpu.make_async_copy(weights_hbm, weights, load_sem.at[3]),
     ]
-    for load in loads:
-        load.start()
+    for i in (1, 2, 0, 3):
+        loads[i].start()
 
     barrier = pltpu.get_barrier_semaphore()
     sp_peers = [far, diag, near]
@@ -77,14 +77,6 @@
         pl.semaphore_signal(barrier, inc=1, device_id=(rep, peer), device_id_type=MESH)
     for peer in (twin, first, second):
         pl.semaphore_signal(barrier, inc=1, device_id=(peer, me), device_id_type=MESH)
-
-    loads[0].wait()
-    wide[...] = field[...].astype(jnp.float32).reshape(wide.shape)
-
-    def block_for(d, j):
-        block = wide[pl.ds(lists[0, d, j], channels, stride=blocks), :]
-        block = jnp.where(j < counts[0, d], block, jnp.zeros_like(block))
-        return block.astype(jnp.bfloat16)
 
     def send(src, dst, ssem, rsem, device):
         copy = pltpu.make_async_remote_copy(
@@ -94,55 +86,69 @@
         copy.start()
         return copy
 
-    a2a = []
-    for k, peer in enumerate(sp_peers):
-        for j in range(slots_each):
-            outgoing[k, j] = block_for(peer, j)
-        if k == 0:
-            pl.semaphore_wait(barrier, 6)
-        a2a.append(send(
-            outgoing.at[k], pool.at[pl.ds(me * slots_each, slots_each)],
-            a2a_send.at[k], a2a_recv.at[k], (rep, peer),
-        ))
-
     def chunk(flip1, flip2):
         return (b1 + flip1 * (1 - 2 * b1)) * w1 + (b2 + flip2 * (1 - 2 * b2)) * w2
 
-    loads[1].wait()
-    loads[2].wait()
-    to_twin = []
-    for k, (f1, f2) in enumerate(((1, 1), (0, 1), (1, 0), (0, 0))):
-        q = chunk(f1, f2)
+    c_both, c_first, c_second, c_none = chunk(1, 1), chunk(1, 0), chunk(0, 1), chunk(0, 0)
+    order = [diag, far, near, me]
+    to_twin, out2, out3, a2a = [], [], [], []
+
+    def product(k, q):
         columns = pl.ds(pl.multiple_of(q * width, 128), width)
         value = lax.dot_general(
             edge[:, columns], cot[...], (((0,), (0,)), ((), ())),
             preferred_element_type=jnp.float32,
         )
         part[q] = value.reshape(part.shape[1:])
+        if k == 0:
+            pl.semaphore_wait(barrier, 6)
         to_twin.append(send(
             part.at[q, 1 - core], got1.at[k], s1.at[k], r1.at[k], (twin, me)
         ))
-    for j in range(slots_each):
-        pool[me * slots_each + j] = block_for(me, j)
-
-    order = [diag, near, far, me]
-    c_both, c_first, c_second, c_none = chunk(1, 1), chunk(1, 0), chunk(0, 1), chunk(0, 0)
+
+    def block_for(d, j):
+        block = wide[pl.ds(lists[0, d, j], channels, stride=blocks), :]
+        block = jnp.where(j < counts[0, d], block, jnp.zeros_like(block))
+        return block.astype(jnp.bfloat16)
+
+    def send_blocks_to(k):
+        peer = sp_peers[k]
+        for j in range(slots_each):
+            outgoing[k, j] = block_for(peer, j)
+        a2a.append(send(
+            outgoing.at[k], pool.at[pl.ds(me * slots_each, slots_each)],
+            a2a_send.at[k], a2a_recv.at[k], (rep, peer),
+        ))
 
     def fold(q, k):
         to_twin[k].wait_recv()
         part[q, core] = part[q, core] + got1[k]
 
-    out2 = []
-    for k, q in enumerate((c_both, c_first)):
+    def send_first(k, q):
         fold(q, k)
         for i in range(4):
             out2.append(send(
                 part.at[q, core, order[i]], got2.at[k, order[i]],
                 s2.at[k, i], r2.at[k, i], (first, me),
             ))
+
+    loads[1].wait()
+    loads[2].wait()
+    product(0, c_both)
+    product(1, c_second)
+    loads[0].wait()
+    wide[...] = field[...].astype(jnp.float32).reshape(wide.shape)
+    send_blocks_to(0)
+    send_first(0, c_both)
+    product(2, c_first)
+    send_blocks_to(1)
+    send_first(1, c_first)
+    send_blocks_to(2)
+    product(3, c_none)
+    for j in range(slots_each):
+        pool[me * slots_each + j] = block_for(me, j)
     fold(c_second, 2)
     fold(c_none, 3)
-    out3 = []
     for i in range(4):
         out2[i].wait_recv()
         part[c_second, core, order[i]] = part[c_second, core, order[i]] + got2[0, order[i]]
@@ -156,13 +162,15 @@
         out3[i].wait_recv()
         total = part[c_none, core, order[i]] + got2[1, order[i]] + got3[order[i]]
         part[c_none, core, order[i]] = total
-        if i < 2:
+        if i in (0, 2):
+            k = len(outz)
             outz.append(send(
-                part.at[c_none, core, order[i]], gotz.at[i], sz.at[i], rz.at[i], (rep, near)
+                part.at[c_none, core, order[i]], gotz.at[k], sz.at[k], rz.at[k], (rep, near)
             ))
-    outz[0].wait_recv()
-    part[c_none, core, far] = part[c_none, core, far] + gotz[0]
-    last = send(part.at[c_none, core, far], gotf, sf, rf, (rep, far))
+        if i == 2:
+            outz[0].wait_recv()
+            part[c_none, core, far] = part[c_none, core, far] + gotz[0]
+            last = send(part.at[c_none, core, far], gotf, sf, rf, (rep, far))
 
     for copy in a2a:
         copy.wait_recv()

time: 34.3 us -> 35.5 us (1.035)
  Pallas kernels: 31.6 us -> 32.8 us
    pallas_call x1, Pallas kernels: 30.9 us -> 32.1 us  [fused(): pl.pallas_call(kernel, out_shape=out_shape, in_specs=[smem, smem, smem, f...]
where the time goes in v3:
time: 35.5 us; the launch traced here: 35.3 us
  Pallas kernels  32.8 us (92%)
  local copies, waits for them, and re-layouts  1.82 us (5%)
  between operations  0.65 us (2%)
    pallas_call x1, Pallas kernels, fused(): pl.pallas_call(kernel, out_shape=out_shape, in_specs=[smem, smem, smem, f...  32.1 us
    unnamed x4, local copies, waits for them, and re-layouts  1.82 us
    pallas_call x1, Pallas kernels, fused(): pl.pallas_call(settle, out_shape=out_shape, in_specs=[near, near], out_sp...  0.73 us

profile of v3, /device:TPU:0, one launch (start us, length us, event | category | flops | bytes accessed | tf_op | source)
XLA Modules:
  0.0 35.3 jit_solution(9152273809467946645)
XLA Ops:
  0.6 32.1 %shard_map.86 = (bf16[1,100,8,128]{3,2,1,0:T(8,128)(2,1)}, f32[48,512]{1,0:T(8,128)}) custom-call(s32[1,4,8]{2,1,0:T(4,128)} %lists.1, s32[1,4]{1,0:T(1,128)} %counts.1, s32[8,8]{1,0:T(8,128)} %slots.1, bf16[1,100,32,128]{3,2,1,0:T(8,128)(2,1)} %bitcast.2, bf16[8,8,128,128]{3,2,1,0:T(8,128)(2,1)} %weights_hbm.1, bf16[384,1536]{1,0:T(8,128)(2,1)} %edge_hbm.1, ...), custom_call_target="tpu_custom_call" | custom-call | tf_op jit(solution)/shard_map/pallas_call | solution.py:215
  32.7 0.0 copy-start
  32.8 0.9 %copy-done = bf16[1,100,8,128]{3,2,1,0:T(8,128)(2,1)S(1)} copy-done((bf16[1,100,8,128]{3,2,1,0:T(8,128)(2,1)S(1)}, bf16[1,100,8,128]{3,2,1,0:T(8,128)(2,1)}, u32[]{:S(2)}) %copy-start) | copy-done | bytes 204824
  33.7 0.0 copy-start.1
  33.7 0.9 %copy-done.1 = f32[48,512]{1,0:T(8,128)S(1)} copy-done((f32[48,512]{1,0:T(8,128)S(1)}, f32[48,512]{1,0:T(8,128)}, u32[]{:S(2)}) %copy-start.1) | copy-done | bytes 98328
  34.6 0.7 %shard_map.87 = (bf16[1,100,8,128]{3,2,1,0:T(8,128)(2,1)}, f32[48,512]{1,0:T(8,128)}) custom-call(bf16[1,100,8,128]{3,2,1,0:T(8,128)(2,1)S(1)} %copy-done, f32[48,512]{1,0:T(8,128)S(1)} %copy-done.1), custom_call_target="tpu_custom_call" | custom-call | tf_op jit(solution)/shard_map/pallas_call | solution.py:250
Async XLA Ops:
  32.7 0.9 %copy-start = (bf16[1,100,8,128]{3,2,1,0:T(8,128)(2,1)S(1)}, bf16[1,100,8,128]{3,2,1,0:T(8,128)(2,1)}, u32[]{:S(2)}) copy-start(bf16[1,100,8,128]{3,2,1,0:T(8,128)(2,1)} %get-tuple-element.6.hidden) | copy-start | bytes 614404
  33.7 0.9 %copy-start.1 = (f32[48,512]{1,0:T(8,128)S(1)}, f32[48,512]{1,0:T(8,128)}, u32[]{:S(2)}) copy-start(f32[48,512]{1,0:T(8,128)} %get-tuple-element.7.grad) | copy-start | bytes 294916
